TPU v7x, 32 devices: a whole 2x2x4 slice. The times are simulated.
32 devices in a mesh: seq: 8 (over z, y), head: 4 (over x, core).
Axes of the slice: x: 2, y: 2, z: 4, core: 2. Of those that a mesh axis runs over, the one named last changes fastest.
Arguments:
- inputs: bfloat16 [2048, 5120], P('seq', 'head'), may hold values from -6 to 6
- time_step: float32 [80, 2048], P('head', 'seq'), may hold values from 0.01 to 0.3
- decay_rate: float32 [80], P('head'), may hold values from 0.0001 to 1
- input_map: bfloat16 [2048, 128], P('seq'), may hold values from -6 to 6
- output_map: bfloat16 [2048, 128], P('seq'), may hold values from -0.59765625 to 0.59765625
- output_grad: bfloat16 [2048, 5120], P('seq', 'head'), may hold values from -3 to 3
- span_states: float32 [8, 80, 64, 128], P('seq', 'head'), may hold values from -6 to 6
- resets: int32 [8], P('seq'), may hold values from 0 to 4095
Outputs:
- grad_inputs: bfloat16 [2048, 5120], P('seq', 'head')
- grad_input_map: float32 [2048, 128], P('seq')
- grad_rate: float32 [80], P('head')
Inputs may be any that keep to these rules, and one draw needn't show every extreme that they name: `resets`: A value p under 256 means that a document starts at position p of that span; a value of 256 or more means that none starts in it.
All inputs are finite; a program needn't handle non-finite values.
Results may differ from a plain program's by a relative error of at most 0.003.
Values sent between devices are 32-bit elements; how exact they have to be, the bound alone decides.
A program may use at most 64 MiB of HBM per device.

v0:
```python
import jax
import jax.numpy as jnp
from jax import lax
from jax.sharding import PartitionSpec as P

highest = lax.Precision.HIGHEST


def prepare(x_block, step_block, decay_rate, b_block, c_block, grad_block, start_state, reset_at):
    block_len = step_block.shape[1]
    positions = jnp.arange(block_len, dtype=jnp.int32)
    later_doc = positions >= reset_at
    no_reset = reset_at >= block_len
    elapsed = jnp.cumsum(step_block, axis=1)
    log_decay = -decay_rate[:, None] * elapsed
    joined = (later_doc[:, None] == later_doc[None, :]) & (positions[None, :] >= positions[:, None])
    log_gaps = log_decay[:, None, :] - log_decay[:, :, None]
    pair_weight = jnp.where(joined[None], jnp.exp(jnp.where(joined[None], log_gaps, 0.0)), 0.0)
    intersection = jnp.dot(b_block, c_block.T, preferred_element_type=jnp.float32)
    products = jnp.einsum("shp,uhp->hsu", x_block, grad_block, preferred_element_type=jnp.float32)
    mixing = (pair_weight * intersection[None]).astype(jnp.bfloat16)
    pair_terms = pair_weight * products
    paired = pair_terms.astype(jnp.bfloat16)
    dx_inner = jnp.einsum("hsu,uhp->shp", mixing, grad_block, preferred_element_type=jnp.float32)
    db_inner = jnp.einsum("hsu,un->hsn", paired, c_block, preferred_element_type=jnp.float32)
    start_weight = jnp.where(later_doc[None], 0.0, jnp.exp(log_decay))
    end_weight = jnp.where(
        (later_doc | no_reset)[None], jnp.exp(log_decay[:, -1:] - log_decay), 0.0
    )
    carry_gain = jnp.where(no_reset, jnp.exp(log_decay[:, -1]), 0.0)
    c_wide = c_block.astype(jnp.float32)
    grad_wide = grad_block.astype(jnp.float32)
    weighted_c = start_weight[:, :, None] * c_wide[None]
    boundary_grad = jnp.einsum("hun,uhp->hpn", weighted_c, grad_wide, precision=highest)
    state_read = jnp.einsum("uhp,hpn->hun", grad_wide, start_state, precision=highest)
    start_term = jnp.sum(state_read * c_wide[None], axis=2)
    inside_term = jnp.sum(
        pair_terms
        * intersection[None]
        * step_block[:, :, None]
        * (elapsed[:, None, :] - elapsed[:, :, None]),
        axis=(1, 2),
    )
    entry_term = jnp.sum(start_weight * elapsed * start_term, axis=1)
    return (
        carry_gain,
        boundary_grad,
        dx_inner,
        db_inner,
        inside_term + entry_term,
        end_weight,
        elapsed,
    )


def finish(prepared, x_block, step_block, b_block, start_state, carried):
    carry_gain, boundary_grad, dx_inner, db_inner, partial_rate, end_weight, elapsed = prepared
    b_wide = b_block.astype(jnp.float32)
    x_wide = x_block.astype(jnp.float32)
    carried_b = jnp.einsum("sn,hpn->shp", b_wide, carried, precision=highest)
    carried_x = jnp.einsum("shp,hpn->hsn", x_wide, carried, precision=highest)
    step_rows = step_block.T[:, :, None]
    end_rows = end_weight.T[:, :, None]
    grad_x = (step_rows * (dx_inner + end_rows * carried_b)).astype(jnp.bfloat16)
    grad_b = jnp.sum(
        step_block[:, :, None] * (db_inner + end_weight[:, :, None] * carried_x), axis=0
    )
    last_elapsed = elapsed[:, -1]
    leaving_term = jnp.sum(
        end_weight
        * step_block
        * (last_elapsed[:, None] - elapsed)
        * jnp.sum(carried_x * b_wide[None], axis=2),
        axis=1,
    )
    through_term = carry_gain * last_elapsed * jnp.sum(carried * start_state, axis=(1, 2))
    return (grad_x, grad_b, partial_rate + leaving_term + through_term)


def backward_step(running, members):
    grad_piece, gain_piece = members
    return (grad_piece + gain_piece[:, None] * running, running)


def body(inputs, time_step, decay_rate, input_map, output_map, output_grad, span_states, resets):
    length = time_step.shape[1]
    block_count = span_states.shape[0]
    block_len = length // block_count
    head_count = decay_rate.shape[0]
    head_width = inputs.shape[1] // head_count
    number = 0
    x_block = inputs.reshape(block_len, head_count, head_width)
    grad_block = output_grad.reshape(block_len, head_count, head_width)
    step_block = time_step
    b_block = input_map
    prepared = prepare(
        x_block,
        step_block,
        decay_rate,
        b_block,
        output_map,
        grad_block,
        span_states[number],
        resets[number],
    )
    pieces = [(prepared, x_block, step_block, b_block)]
    gain_total = jnp.ones((head_count,), jnp.float32)
    grad_total = jnp.zeros_like(span_states[0])
    for number in reversed(range(block_count)):
        gain_block, grad_block_sum = (pieces[number][0][0], pieces[number][0][1])
        grad_total = grad_block_sum + gain_block[:, None, None] * grad_total
        gain_total = gain_block * gain_total
    seq_count = lax.axis_size("seq")
    entries = grad_total.shape[1] * grad_total.shape[2]
    sliced = grad_total.reshape(head_count, seq_count, entries // seq_count)
    received = lax.all_to_all(sliced, "seq", split_axis=1, concat_axis=1, tiled=True)
    gains = lax.all_gather(gain_total[None], "seq", axis=0, tiled=True)
    ending, exclusive = lax.scan(
        backward_step,
        jnp.zeros_like(received[:, 0]),
        (jnp.transpose(received, (1, 0, 2)), gains),
        reverse=True,
    )
    returned = lax.all_to_all(
        jnp.transpose(exclusive, (1, 0, 2)), "seq", split_axis=1, concat_axis=1, tiled=True
    )
    incoming = returned.reshape(grad_total.shape)
    carried = incoming
    grad_x_list = [None] * block_count
    grad_b_list = [None] * block_count
    rate_total = jnp.zeros((head_count,), jnp.float32)
    for number in reversed(range(block_count)):
        prepared, x_block, step_block, b_block = pieces[number]
        grad_x, grad_b, rate_part = finish(
            prepared, x_block, step_block, b_block, span_states[number], carried
        )
        grad_x_list[number] = grad_x.reshape(block_len, head_count * head_width)
        grad_b_list[number] = grad_b
        rate_total = rate_part
        carried = prepared[1] + prepared[0][:, None, None] * carried
    grad_inputs = grad_x_list[0]
    grad_input_map = lax.psum(grad_b_list[0], "head")
    grad_rate = -lax.psum(rate_total, "seq")
    return (grad_inputs, grad_input_map, grad_rate)


def solution(mesh):
    in_specs = (
        P("seq", "head"),
        P("head", "seq"),
        P("head"),
        P("seq", None),
        P("seq", None),
        P("seq", "head"),
        P("seq", "head", None, None),
        P("seq"),
    )
    out_specs = (P("seq", "head"), P("seq", None), P("head"))
    return jax.shard_map(body, mesh=mesh, in_specs=in_specs, out_specs=out_specs, check_vma=False)
```

profile of v0, /device:TPU:0, one launch (start us, length us, event | category | flops | bytes accessed | tf_op | source)
XLA Modules:
  0.0 141.0 jit_solution(17333116644024165966)
XLA Ops:
  8.6 0.8 reshape.290
  11.2 0.9 copy.37
  12.2 1.4 copy.36
  13.6 1.7 %fusion.31 = f32[20,64,128]{2,1,0:T(8,128)S(1)} fusion(bf16[256,20,64]{0,2,1:T(8,128)(2,1)S(1)} %bitcast.80, f32[256,128]{0,1:T(8,128)S(1)} %copy.37, f32[20,256]{1,0:T(8,128)S(1)} %get-tuple-element.152, f32[20]{0:T(128)S(1)} %broadcast_multiply_fusion.1), kind=kOutput, calls=%fused_computation.38 | convolution fusion | flops 504135680 | bytes 1462352 | tf_op jit(solution)/shard_map/hun,uhp->hpn/dot_general | solution.py:34
  15.4 1.3 copy.39
  16.7 7.3 %all-to-all-start = ((f32[20,8,1024]{2,0,1:T(8,128)}), f32[20,8,1024]{2,0,1:T(8,128)S(1)}, u32[]{:S(2)}, u32[]{:S(2)}) async-start(f32[20,8,1024]{2,0,1:T(8,128)} %copy.39), calls=%async_computation | async-start | bytes 1572864 | tf_op jit(solution)/shard_map/all_to_all | solution.py:116
  25.6 26.1 %all-reduce = f32[160]{0:T(256)S(1)} all-reduce(f32[160]{0:T(256)S(1)} %dynamic-update-slice), channel_id=2, replica_groups=mesh['seq'=8,'head'=4] {'seq'}, use_global_device_ids=true, to_apply=%add | all-reduce | flops 160 | bytes 1280
  53.9 0.7 slice_reduce_fusion.1
  54.7 1.4 %fusion.37 = pred[256,256]{1,0:T(8,128)(4,1)} fusion(pred[256]{0:T(512)(128)(4,1)} %copy-done.10), kind=kLoop, calls=%fused_computation.42 | loop fusion | flops 196608 | bytes 65792 | tf_op jit(solution)/shard_map/and | solution.py:16
  56.1 1.8 %fusion.43 = f32[256,256]{1,0:T(8,128)} fusion(bf16[256,128]{1,0:T(8,128)(2,1)} %param.13, bf16[256,128]{1,0:T(8,128)(2,1)} %param.14), kind=kOutput, calls=%fused_computation.64 | convolution fusion | flops 16777216 | bytes 393216 | tf_op jit(solution)/shard_map/dot_general | solution.py:19
  57.9 1.0 broadcast_in_dim.97
  58.9 11.4 %while.17 = (s32[]{:T(128)}, f32[20,1024]{1,0:T(8,128)S(1)}, f32[8,20,1024]{2,1,0:T(8,128)}, f32[8,20,1024]{2,1,0:T(8,128)S(1)}, f32[8,20]{1,0:T(8,128)}, /*index=5*/s32[]{:T(128)}, s32[]{:T(128)}, s32[]{:T(128)}) while((s32[]{:T(128)}, f32[20,1024]{1,0:T(8,128)S(1)}, f32[8,20,1024]{2,1,0:T(8,128)}, f32[8,20,1024]{2,1,0:T(8,128)S(1)}, ...), condition=%wide.region_3.4_spmd.clone, body=%wide.region_2.3_spmd.clone.sunk | while | flops 81924 | bytes 426352 | solution.py:118
  60.3 0.7 fusion.55
  61.7 0.7 fusion.55
  63.1 0.7 fusion.55
  64.6 0.7 fusion.55
  66.0 0.7 fusion.55
  67.4 0.7 fusion.55
  68.9 0.7 fusion.55
  70.3 4.5 %all-to-all-start.1 = ((f32[20,8,1024]{2,0,1:T(8,128)}), f32[20,8,1024]{2,0,1:T(8,128)S(1)}, u32[]{:S(2)}, u32[]{:S(2)}) async-start(f32[20,8,1024]{2,0,1:T(8,128)} %bitcast.8), calls=%async_computation.1 | async-start | bytes 1572864 | tf_op jit(solution)/shard_map/all_to_all | solution.py:124
  74.8 2.8 %multiply_reduce_fusion.1 = f32[20,256]{1,0:T(8,128)} fusion(bf16[256,20,64]{0,2,1:T(8,128)(2,1)S(1)} %bitcast.81, f32[256,128]{0,1:T(8,128)} %copy-done.7, f32[1,20,64,128]{3,2,1,0:T(8,128)S(1)} %copy-done.2), kind=kOutput, calls=%fused_computation.17 | convolution fusion | flops 504622080 | bytes 1462272 | tf_op jit(solution)/shard_map/uhp,hpn->hun/dot_general | solution.py:35
  77.7 3.7 %fusion.21 = f32[256,20,64]{0,2,1:T(8,128)} fusion(bf16[256,20,64]{0,2,1:T(8,128)(2,1)S(1)} %bitcast.82, f32[256,256]{1,0:T(8,128)} %fusion.43, f32[20,256]{1,0:T(8,128)S(1)} %get-tuple-element.153, pred[256,256]{1,0:T(8,128)(4,1)} %fusion.37), kind=kOutput, calls=%fused_computation.29 | convolution fusion | flops 174325760 | bytes 2314240 | tf_op jit(solution)/shard_map/hsu,uhp->shp/dot_general | solution.py:24
  81.4 5.3 %multiply_reduce_fusion = (f32[20]{0:T(128)}, f32[20,256,256]{2,1,0:T(8,128)}) fusion(f32[20,256]{1,0:T(8,128)S(1)} %bitcast.86, f32[20,256]{1,0:T(8,128)S(1)} %copy-done.6, f32[256,256]{1,0:T(8,128)S(1)} %copy-done.5, f32[20,256]{1,0:T(8,128)S(1)} %get-tuple-element.153, pred[256,256]{1,0:T(8,128)(4,1)S(1)} %copy-done.8, ...), kind=kOutput, calls=%fused_computation.4 | convolution fusion | flops 179568624 | bytes 6942800 | tf_op jit(solution)/shard_map/shp,uhp->hsu/dot_general | solution.py:20
  86.8 5.5 %all-to-all-done.1 = f32[20,8,1024]{2,0,1:T(8,128)S(1)} async-done(((f32[20,8,1024]{2,0,1:T(8,128)}), f32[20,8,1024]{2,0,1:T(8,128)S(1)}, u32[]{:S(2)}, u32[]{:S(2)}) %all-to-all-start.1) | async-done | bytes 655392 | tf_op jit(solution)/shard_map/all_to_all | solution.py:124
  92.3 1.1 multiply_reduce_fusion.2
  93.4 2.8 %fusion.9 = (f32[20,256]{1,0:T(8,128)S(1)}, f32[20,128,256]{1,2,0:T(8,128)S(1)}) fusion(f32[256,128]{1,0:T(8,128)} %convert_element_type.21, f32[20,64,128]{2,1,0:T(8,128)S(1)} %reshape.294, bf16[256,20,64]{0,2,1:T(8,128)(2,1)S(1)} %bitcast.77), kind=kOutput, calls=%fused_computation.16 | convolution fusion | flops 504622080 | bytes 4083712 | tf_op jit(solution)/shard_map/shp,hpn->hsn/dot_general | solution.py:61
  96.5 5.2 %fusion.8 = f32[256,128]{1,0:T(8,128)} fusion(f32[20,128,256]{1,2,0:T(8,128)S(1)} %get-tuple-element.155, f32[20,256]{1,0:T(8,128)S(1)} %get-tuple-element.150, f32[20,256]{1,0:T(8,128)S(1)} %copy-done.6, f32[20,256,256]{2,1,0:T(8,128)} %get-tuple-element.157, f32[20,256]{1,0:T(8,128)S(1)} %get-tuple-element.153, pred[256,256]{1,0:T(8,128)(4,1)} %fusion.37, ...), kind=kOutput, calls=%fused_computation.15 | convolution fusion | flops 344686592 | bytes 8187904 | tf_op jit(solution)/shard_map/hsu,un->hsn/dot_general | solution.py:25
  101.8 0.7 fusion.25
  102.4 19.4 %psum.15 = f32[20]{0:T(128)S(1)} all-reduce(f32[20]{0:T(128)S(1)} %multiply_add_fusion), channel_id=1, replica_groups=mesh['seq'=8,'head'=4] {'seq'}, use_global_device_ids=true, to_apply=%region_12.13 | all-reduce | flops 20 | bytes 160 | tf_op jit(solution)/shard_map/psum | solution.py:143
  121.8 1.1 copy.44
  123.4 9.1 %all-reduce.3.cloned.1.call-done = f32[256,128]{1,0:T(8,128)} async-done(((f32[256,128]{1,0:T(8,128)}), f32[256,128]{1,0:T(8,128)}) %all-reduce.3.cloned.1.call-update) | async-done | bytes 131088 | tf_op jit(solution)/shard_map/psum | solution.py:142
  132.6 1.6 %copy.62 = f32[256,128]{1,0:T(8,128)} copy(f32[256,128]{1,0:T(8,128)} %all-reduce.3.cloned.1.call-done) | data formatting | bytes 262144
  (90 shorter events, 13.1 us)
Async XLA Ops:
  7.2 16.8 %copy-start.20 = (u32[32]{0:T(128)S(1)}, u32[32]{0:T(128)}, u32[]{:S(2)}) copy-start(u32[32]{0:T(128)} %constant.57) | copy-start | bytes 388
  7.2 45.2 %copy-start.3 = (bf16[256,128]{1,0:T(8,128)(2,1)S(1)}, bf16[256,128]{1,0:T(8,128)(2,1)}, u32[]{:S(2)}) copy-start(bf16[256,128]{1,0:T(8,128)(2,1)} %param.13) | copy-start | bytes 196612
  7.2 45.8 %copy-start.1 = (bf16[256,1280]{1,0:T(8,128)(2,1)S(1)}, bf16[256,1280]{1,0:T(8,128)(2,1)}, u32[]{:S(2)}) copy-start(bf16[256,1280]{1,0:T(8,128)(2,1)} %param.10) | copy-start | bytes 1966084
  7.2 46.0 %copy-start.2 = (f32[1,20,64,128]{3,2,1,0:T(8,128)S(1)}, f32[1,20,64,128]{3,2,1,0:T(8,128)}, u32[]{:S(2)}) copy-start(f32[1,20,64,128]{3,2,1,0:T(8,128)} %param.16) | copy-start | bytes 1966084
  8.6 43.7 %copy-start.14 = (f32[20]{0:T(128)}, f32[20]{0:T(128)S(1)}, u32[]{:S(2)}) copy-start(f32[20]{0:T(128)S(1)} %neg.7) | copy-start | bytes 244
  10.9 41.4 %copy-start.10 = (pred[256]{0:T(512)(128)(4,1)}, pred[256]{0:T(512)(128)(4,1)S(1)}, u32[]{:S(2)}) copy-start(pred[256]{0:T(512)(128)(4,1)S(1)} %get-tuple-element.158) | copy-start | bytes 772
  11.2 41.1 %copy-start.11 = (f32[20]{0:T(128)}, f32[20]{0:T(128)S(1)}, u32[]{:S(2)}) copy-start(f32[20]{0:T(128)S(1)} %get-tuple-element.137) | copy-start | bytes 244
  12.2 1.4 copy-start.7
  16.7 41.2 %all-to-all-start = ((f32[20,8,1024]{2,0,1:T(8,128)}), f32[20,8,1024]{2,0,1:T(8,128)S(1)}, u32[]{:S(2)}, u32[]{:S(2)}) async-start(f32[20,8,1024]{2,0,1:T(8,128)} %copy.39), calls=%async_computation | async-start | bytes 1572864 | tf_op jit(solution)/shard_map/all_to_all | solution.py:116
  70.3 22.0 %all-to-all-start.1 = ((f32[20,8,1024]{2,0,1:T(8,128)}), f32[20,8,1024]{2,0,1:T(8,128)S(1)}, u32[]{:S(2)}, u32[]{:S(2)}) async-start(f32[20,8,1024]{2,0,1:T(8,128)} %bitcast.8), calls=%async_computation.1 | async-start | bytes 1572864 | tf_op jit(solution)/shard_map/all_to_all | solution.py:124
  74.8 57.8 %all-reduce.3.cloned.1.call-start = ((), (), s32[]{:S(2)}) async-start(), calls=%async_computation.2 | async-start | bytes 262144 | tf_op jit(solution)/shard_map/psum | solution.py:142
  77.7 3.7 %copy-start.5 = (f32[256,256]{1,0:T(8,128)S(1)}, f32[256,256]{1,0:T(8,128)}, u32[]{:S(2)}) copy-start(f32[256,256]{1,0:T(8,128)} %fusion.43) | copy-start | bytes 786436
  77.7 3.7 %copy-start.6 = (f32[20,256]{1,0:T(8,128)S(1)}, f32[20,256]{1,0:T(8,128)}, u32[]{:S(2)}) copy-start(f32[20,256]{1,0:T(8,128)} %param.11) | copy-start | bytes 61444
  77.7 3.7 %copy-start.8 = (pred[256,256]{1,0:T(8,128)(4,1)S(1)}, pred[256,256]{1,0:T(8,128)(4,1)}, u32[]{:S(2)}) copy-start(pred[256,256]{1,0:T(8,128)(4,1)} %fusion.37) | copy-start | bytes 196612
  86.8 9.4 %copy-start.9 = (f32[20,256]{1,0:T(8,128)S(1)}, f32[20,256]{1,0:T(8,128)}, u32[]{:S(2)}) copy-start(f32[20,256]{1,0:T(8,128)} %multiply_reduce_fusion.1) | copy-start | bytes 61444
  86.8 9.4 %copy-start.12 = (f32[20]{0:T(128)S(1)}, f32[20]{0:T(128)}, u32[]{:S(2)}) copy-start(f32[20]{0:T(128)} %copy-done.11) | copy-start | bytes 244
  86.8 9.5 %copy-start.13 = (f32[20]{0:T(128)S(1)}, f32[20]{0:T(128)}, u32[]{:S(2)}) copy-start(f32[20]{0:T(128)} %slice_reduce_fusion.1) | copy-start | bytes 244
  86.8 9.5 %copy-start.15 = (f32[20]{0:T(128)S(1)}, f32[20]{0:T(128)}, u32[]{:S(2)}) copy-start(f32[20]{0:T(128)} %copy-done.14) | copy-start | bytes 244
  86.8 9.5 %copy-start.16 = (pred[256]{0:T(512)(128)(4,1)S(1)}, pred[256]{0:T(512)(128)(4,1)}, u32[]{:S(2)}) copy-start(pred[256]{0:T(512)(128)(4,1)} %get-tuple-element.159) | copy-start | bytes 772
  86.8 9.5 %copy-start.18 = (pred[256]{0:T(512)(128)(4,1)S(1)}, pred[256]{0:T(512)(128)(4,1)}, u32[]{:S(2)}) copy-start(pred[256]{0:T(512)(128)(4,1)} %compare_bitcast_fusion) | copy-start | bytes 772
  96.5 5.2 %copy-start.17 = (f32[20]{0:T(128)S(1)}, f32[20]{0:T(128)}, u32[]{:S(2)}) copy-start(f32[20]{0:T(128)} %get-tuple-element.148) | copy-start | bytes 244
  96.5 5.2 %copy-start.19 = (f32[20]{0:T(128)S(1)}, f32[20]{0:T(128)}, u32[]{:S(2)}) copy-start(f32[20]{0:T(128)} %get-tuple-element.156) | copy-start | bytes 244
  96.5 5.2 %copy-start = (f32[256,20,64]{0,2,1:T(8,128)S(1)}, f32[256,20,64]{0,2,1:T(8,128)}, u32[]{:S(2)}) copy-start(f32[256,20,64]{0,2,1:T(8,128)} %fusion.21) | copy-start | bytes 3932164
  96.5 5.2 %copy-start.4 = (bf16[256,128]{1,0:T(8,128)(2,1)S(1)}, bf16[256,128]{1,0:T(8,128)(2,1)}, u32[]{:S(2)}) copy-start(bf16[256,128]{1,0:T(8,128)(2,1)} %param.13) | copy-start | bytes 196612
Sparse Core Ops, SparseCore 0:
  101.8 30.7 all-reduce.2
where the time goes:
time: 142 us; the launch traced here: 141 us
  blocking collectives  45.5 us (32%)
  matrix products  24 us (17%)
  local copies, waits for them, and re-layouts  16.6 us (12%)
  between operations  15.8 us (11%)
  waiting for transfers between devices  14.6 us (10%)
  other arithmetic  12.4 us (9%)
  starting transfers between devices  11.9 us (8%)
    unnamed x1, blocking collectives  26.1 us
    psum x1, blocking collectives, body(): grad_rate = -lax.psum(rate_total, 'seq')  19.4 us
    psum x1, waiting for transfers between devices, body(): grad_input_map = lax.psum(grad_b_list[0], 'head')  9.15 us
    all_to_all x1, starting transfers between devices, body(): lax.all_to_all(sliced, 'seq', split_axis=1, concat_axis=1, tiled=True)  7.31 us
    mul x8, local copies, waits for them, and re-layouts, backward_step(): return (grad_piece + gain_piece[:, None] * running, running)  5.48 us
    all_to_all x1, waiting for transfers between devices, body(): lax.all_to_all(jnp.transpose(exclusive, (1, 0, 2)), 'seq', split_axis=1,...  5.48 us
    dot_general x1, matrix products, prepare(): jnp.einsum('shp,uhp->hsu', x_block, grad_block, preferred_element_type=jn...  5.34 us
    unnamed x51, local copies, waits for them, and re-layouts  5.26 us
  transfers between devices with their start and end apart: 3, of which 2 were waited for; matrix products, arithmetic and copies ran while one was open for 15% of the time, Pallas kernels for 0%

commit v1 on v0

--- a/solution.py
+++ b/solution.py
@@ -139,7 +139,7 @@
         rate_total = rate_part
         carried = prepared[1] + prepared[0][:, None, None] * carried
     grad_inputs = grad_x_list[0]
-    grad_input_map = lax.psum(grad_b_list[0], "head")
+    grad_input_map = jnp.sum(lax.all_gather(grad_b_list[0], "head"), axis=0)
     grad_rate = -lax.psum(rate_total, "seq")
     return (grad_inputs, grad_input_map, grad_rate)
 

time: 142 us -> 130 us (0.915)
  between operations: 15.8 us -> 2.25 us
  waiting for transfers between devices: 14.6 us -> 5.55 us
  blocking collectives: 45.5 us -> 51.4 us
  other arithmetic: 12.4 us -> 15.3 us
  matrix products: 24 us -> 26.5 us
    psum x1 -> x0, waiting for transfers between devices: 9.15 us -> none  [body(): grad_input_map = lax.psum(grad_b_list[0], 'head')]
    all_gather x0 -> x1, blocking collectives: none -> 7.17 us  [body(): grad_input_map = jnp.sum(lax.all_gather(grad_b_list[0], 'head'), axis=0)]
    unnamed x51 -> x40, local copies, waits for them, and re-layouts: 5.26 us -> 4.94 us
  transfers between devices with their start and end apart: 3 -> 2, of which waited for: 2 -> 1; matrix products, arithmetic and copies ran while one was open for 15% -> 16% of each run, Pallas kernels for 0% -> 0%
where the time goes in v1:
time: 130 us; the launch traced here: 129 us
  blocking collectives  51.4 us (40%)
  matrix products  26.5 us (20%)
  local copies, waits for them, and re-layouts  16.3 us (13%)
  other arithmetic  15.3 us (12%)
  starting transfers between devices  11.8 us (9%)
  waiting for transfers between devices  5.55 us (4%)
  between operations  2.25 us (2%)
    unnamed x1, blocking collectives  24.8 us
    psum x1, blocking collectives, body(): grad_rate = -lax.psum(rate_total, 'seq')  19.4 us
    all_to_all x1, starting transfers between devices, body(): lax.all_to_all(sliced, 'seq', split_axis=1, concat_axis=1, tiled=True)  7.31 us
    all_gather x1, blocking collectives, body(): grad_input_map = jnp.sum(lax.all_gather(grad_b_list[0], 'head'), axis=0)  7.17 us
    all_to_all x1, waiting for transfers between devices, body(): lax.all_to_all(jnp.transpose(exclusive, (1, 0, 2)), 'seq', split_axis=1,...  5.55 us
    mul x8, local copies, waits for them, and re-layouts, backward_step(): return (grad_piece + gain_piece[:, None] * running, running)  5.46 us
    dot_general x1, matrix products, prepare(): jnp.einsum('hsu,un->hsn', paired, c_block, preferred_element_type=jnp.flo...  5.42 us
    dot_general x1, matrix products, prepare(): jnp.einsum('shp,uhp->hsu', x_block, grad_block, preferred_element_type=jn...  5.34 us
  transfers between devices with their start and end apart: 2, of which 1 were waited for; matrix products, arithmetic and copies ran while one was open for 16% of the time, Pallas kernels for 0%

profile of v1, /device:TPU:0, one launch (start us, length us, event | category | flops | bytes accessed | tf_op | source)
XLA Modules:
  0.0 129.3 jit_solution(13751108665343851605)
XLA Ops:
  2.1 0.8 reshape.290
  4.4 0.8 select_reduce_fusion
  5.2 0.9 copy.48
  6.2 1.4 %copy.47 = bf16[256,1280]{0,1:T(8,128)(2,1)S(1)} copy(bf16[256,1280]{1,0:T(8,128)(2,1)} %param.15) | data formatting | bytes 1310720 | tf_op args[5]
  7.6 1.7 %fusion.31 = f32[20,64,128]{2,1,0:T(8,128)S(1)} fusion(bf16[256,20,64]{0,2,1:T(8,128)(2,1)S(1)} %bitcast.82, f32[256,128]{0,1:T(8,128)S(1)} %copy.48, f32[20,256]{1,0:T(8,128)S(1)} %get-tuple-element.155, f32[20]{0:T(128)S(1)} %broadcast_multiply_fusion.1), kind=kOutput, calls=%fused_computation.38 | convolution fusion | flops 504135680 | bytes 1462352 | tf_op jit(solution)/shard_map/hun,uhp->hpn/dot_general | solution.py:34
  9.4 1.3 copy.50
  10.7 7.3 %all-to-all-start = ((f32[20,8,1024]{2,0,1:T(8,128)}), f32[20,8,1024]{2,0,1:T(8,128)S(1)}, u32[]{:S(2)}, u32[]{:S(2)}) async-start(f32[20,8,1024]{2,0,1:T(8,128)} %copy.50), calls=%async_computation | async-start | bytes 1572864 | tf_op jit(solution)/shard_map/all_to_all | solution.py:116
  18.0 1.3 %dynamic-slice = u32[1]{0:T(128)} dynamic-slice(u32[32]{0:T(128)} %constant.57, u32[]{:T(128)S(6)} %add.58), dynamic_slice_sizes={1} | dynamic-slice | bytes 12
  20.0 0.9 dynamic-update-slice
  20.8 24.8 %all-reduce = f32[160]{0:T(256)S(1)} all-reduce(f32[160]{0:T(256)S(1)} %dynamic-update-slice), channel_id=2, replica_groups=mesh['seq'=8,'head'=4] {'seq'}, use_global_device_ids=true, to_apply=%add | all-reduce | flops 160 | bytes 1280
  46.3 1.5 %convert_element_type.21 = f32[256,128]{1,0:T(8,128)} convert(bf16[256,128]{1,0:T(8,128)(2,1)} %param.13) | non-fusion elementwise | flops 32768 | bytes 196608 | tf_op jit(solution)/shard_map/convert_element_type | solution.py:58
  48.8 0.8 slice_reduce_fusion.1
  49.5 1.5 %fusion.37 = pred[256,256]{1,0:T(8,128)(4,1)} fusion(pred[256]{0:T(512)(128)(4,1)} %copy-done.9), kind=kLoop, calls=%fused_computation.42 | loop fusion | flops 196608 | bytes 65792 | tf_op jit(solution)/shard_map/and | solution.py:16
  51.0 1.8 %fusion.43 = f32[256,256]{1,0:T(8,128)} fusion(bf16[256,128]{1,0:T(8,128)(2,1)} %param.13, bf16[256,128]{1,0:T(8,128)(2,1)} %param.14), kind=kOutput, calls=%fused_computation.64 | convolution fusion | flops 16777216 | bytes 393216 | tf_op jit(solution)/shard_map/dot_general | solution.py:19
  52.8 1.0 broadcast_in_dim.97
  53.8 11.4 %while.17 = (s32[]{:T(128)}, f32[20,1024]{1,0:T(8,128)S(1)}, f32[8,20,1024]{2,1,0:T(8,128)}, f32[8,20,1024]{2,1,0:T(8,128)S(1)}, f32[8,20]{1,0:T(8,128)}, /*index=5*/s32[]{:T(128)}, s32[]{:T(128)}, s32[]{:T(128)}) while((s32[]{:T(128)}, f32[20,1024]{1,0:T(8,128)S(1)}, f32[8,20,1024]{2,1,0:T(8,128)}, f32[8,20,1024]{2,1,0:T(8,128)S(1)}, ...), condition=%wide.region_3.4_spmd.clone, body=%wide.region_2.3_spmd.clone.sunk | while | flops 81924 | bytes 426352 | solution.py:118
  55.2 0.7 fusion.55
  56.6 0.7 fusion.55
  60.9 0.7 fusion.55
  65.2 4.5 %all-to-all-start.1 = ((f32[20,8,1024]{2,0,1:T(8,128)}), f32[20,8,1024]{2,0,1:T(8,128)S(1)}, u32[]{:S(2)}, u32[]{:S(2)}) async-start(f32[20,8,1024]{2,0,1:T(8,128)} %bitcast.8), calls=%async_computation.1 | async-start | bytes 1572864 | tf_op jit(solution)/shard_map/all_to_all | solution.py:124
  69.7 2.8 %multiply_reduce_fusion.1 = f32[20,256]{1,0:T(8,128)} fusion(bf16[256,20,64]{0,2,1:T(8,128)(2,1)S(1)} %bitcast.83, f32[256,128]{0,1:T(8,128)} %copy-done.6, f32[1,20,64,128]{3,2,1,0:T(8,128)S(1)} %copy-done.1), kind=kOutput, calls=%fused_computation.17 | convolution fusion | flops 504622080 | bytes 1462272 | tf_op jit(solution)/shard_map/uhp,hpn->hun/dot_general | solution.py:35
  72.5 3.7 %fusion.21 = f32[256,20,64]{0,2,1:T(8,128)} fusion(bf16[256,20,64]{0,2,1:T(8,128)(2,1)S(1)} %bitcast.84, f32[256,256]{1,0:T(8,128)} %fusion.43, f32[20,256]{1,0:T(8,128)S(1)} %get-tuple-element.156, pred[256,256]{1,0:T(8,128)(4,1)} %fusion.37), kind=kOutput, calls=%fused_computation.29 | convolution fusion | flops 174325760 | bytes 2314240 | tf_op jit(solution)/shard_map/hsu,uhp->shp/dot_general | solution.py:24
  76.3 5.3 %multiply_reduce_fusion = (f32[20]{0:T(128)}, f32[20,256,256]{2,1,0:T(8,128)}) fusion(f32[20,256]{1,0:T(8,128)S(1)} %bitcast.88, f32[20,256]{1,0:T(8,128)S(1)} %copy-done.5, f32[256,256]{1,0:T(8,128)S(1)} %copy-done.3, f32[20,256]{1,0:T(8,128)S(1)} %get-tuple-element.156, pred[256,256]{1,0:T(8,128)(4,1)S(1)} %copy-done.7, ...), kind=kOutput, calls=%fused_computation.4 | convolution fusion | flops 179568624 | bytes 6942800 | tf_op jit(solution)/shard_map/shp,uhp->hsu/dot_general | solution.py:20
  81.6 5.5 %all-to-all-done.1 = f32[20,8,1024]{2,0,1:T(8,128)S(1)} async-done(((f32[20,8,1024]{2,0,1:T(8,128)}), f32[20,8,1024]{2,0,1:T(8,128)S(1)}, u32[]{:S(2)}, u32[]{:S(2)}) %all-to-all-start.1) | async-done | bytes 655392 | tf_op jit(solution)/shard_map/all_to_all | solution.py:124
  87.2 1.1 multiply_reduce_fusion.2
  88.3 3.7 %fusion.9 = (f32[20,256]{1,0:T(8,128)S(1)}, f32[20,128,256]{1,2,0:T(8,128)}) fusion(f32[256,128]{1,0:T(8,128)} %convert_element_type.21, f32[20,64,128]{2,1,0:T(8,128)S(1)} %reshape.294, bf16[256,20,64]{0,2,1:T(8,128)(2,1)S(1)} %bitcast.78), kind=kOutput, calls=%fused_computation.16 | convolution fusion | flops 504622080 | bytes 4083712 | tf_op jit(solution)/shard_map/shp,hpn->hsn/dot_general | solution.py:61
  92.0 0.9 multiply_reduce_fusion.4
  93.0 2.0 %fusion.25 = bf16[256,20,64]{0,2,1:T(8,128)(2,1)S(1)} fusion(f32[256,20,64]{0,2,1:T(8,128)} %fusion.21, f32[20,64,128]{2,1,0:T(8,128)S(1)} %reshape.294, f32[256,20]{0,1:T(8,128)S(1)} %get-tuple-element.154, f32[256,20]{0,1:T(8,128)S(1)} %bitcast.90, bf16[256,128]{1,0:T(8,128)(2,1)S(1)} %copy-done.2), kind=kOutput, calls=%fused_computation.34 | convolution fusion | flops 504627200 | bytes 2727936 | tf_op jit(solution)/shard_map/sn,hpn->shp/dot_general | solution.py:60
  95.0 1.1 copy.55
  96.1 19.4 %psum.7 = f32[20]{0:T(128)S(1)} all-reduce(f32[20]{0:T(128)S(1)} %multiply_add_fusion), channel_id=1, replica_groups=mesh['seq'=8,'head'=4] {'seq'}, use_global_device_ids=true, to_apply=%region_12.13 | all-reduce | flops 20 | bytes 160 | tf_op jit(solution)/shard_map/psum | solution.py:143
  116.0 5.4 %fusion.8 = f32[256,128]{1,0:T(8,128)S(1)} fusion(f32[20,128,256]{1,2,0:T(8,128)} %get-tuple-element.158, f32[20,256]{1,0:T(8,128)S(1)} %get-tuple-element.153, f32[20,256]{1,0:T(8,128)S(1)} %copy-done.5, f32[20,256,256]{2,1,0:T(8,128)} %get-tuple-element.160, f32[20,256]{1,0:T(8,128)S(1)} %get-tuple-element.156, pred[256,256]{1,0:T(8,128)(4,1)S(1)} %copy-done.8, ...), kind=kOutput, calls=%fused_computation.15 | convolution fusion | flops 344686592 | bytes 8187904 | tf_op jit(solution)/shard_map/hsu,un->hsn/dot_general | solution.py:25
  121.4 7.2 %all-gather.1 = f32[1024,128]{1,0:T(8,128)S(1)} all-gather(f32[256,128]{1,0:T(8,128)S(1)} %fusion.8), channel_id=3, replica_groups=mesh['seq'=8,'head'=4] {'head'}, dimensions={0}, use_global_device_ids=true | all-gather | bytes 655360 | tf_op jit(solution)/shard_map/all_gather | solution.py:142
  (78 shorter events, 14.5 us)
Async XLA Ops:
  0.6 47.2 %copy-start = (bf16[256,1280]{1,0:T(8,128)(2,1)S(1)}, bf16[256,1280]{1,0:T(8,128)(2,1)}, u32[]{:S(2)}) copy-start(bf16[256,1280]{1,0:T(8,128)(2,1)} %param.10) | copy-start | bytes 1966084
  0.6 47.4 %copy-start.1 = (f32[1,20,64,128]{3,2,1,0:T(8,128)S(1)}, f32[1,20,64,128]{3,2,1,0:T(8,128)}, u32[]{:S(2)}) copy-start(f32[1,20,64,128]{3,2,1,0:T(8,128)} %param.16) | copy-start | bytes 1966084
  2.1 2.4 %copy-start.13 = (f32[20]{0:T(128)}, f32[20]{0:T(128)S(1)}, u32[]{:S(2)}) copy-start(f32[20]{0:T(128)S(1)} %neg.7) | copy-start | bytes 244
  4.3 13.6 %copy-start.9 = (pred[256]{0:T(512)(128)(4,1)}, pred[256]{0:T(512)(128)(4,1)S(1)}, u32[]{:S(2)}) copy-start(pred[256]{0:T(512)(128)(4,1)S(1)} %get-tuple-element.161) | copy-start | bytes 772
  5.2 12.8 %copy-start.10 = (f32[20]{0:T(128)}, f32[20]{0:T(128)S(1)}, u32[]{:S(2)}) copy-start(f32[20]{0:T(128)S(1)} %get-tuple-element.140) | copy-start | bytes 244
  6.2 1.4 %copy-start.6 = (f32[256,128]{0,1:T(8,128)}, f32[256,128]{0,1:T(8,128)S(1)}, u32[]{:S(2)}) copy-start(f32[256,128]{0,1:T(8,128)S(1)} %copy.48) | copy-start | bytes 393220
  10.7 42.1 %all-to-all-start = ((f32[20,8,1024]{2,0,1:T(8,128)}), f32[20,8,1024]{2,0,1:T(8,128)S(1)}, u32[]{:S(2)}, u32[]{:S(2)}) async-start(f32[20,8,1024]{2,0,1:T(8,128)} %copy.50), calls=%async_computation | async-start | bytes 1572864 | tf_op jit(solution)/shard_map/all_to_all | solution.py:116
  65.2 22.0 %all-to-all-start.1 = ((f32[20,8,1024]{2,0,1:T(8,128)}), f32[20,8,1024]{2,0,1:T(8,128)S(1)}, u32[]{:S(2)}, u32[]{:S(2)}) async-start(f32[20,8,1024]{2,0,1:T(8,128)} %bitcast.8), calls=%async_computation.1 | async-start | bytes 1572864 | tf_op jit(solution)/shard_map/all_to_all | solution.py:124
  72.5 3.7 %copy-start.3 = (f32[256,256]{1,0:T(8,128)S(1)}, f32[256,256]{1,0:T(8,128)}, u32[]{:S(2)}) copy-start(f32[256,256]{1,0:T(8,128)} %fusion.43) | copy-start | bytes 786436
  72.5 3.7 %copy-start.5 = (f32[20,256]{1,0:T(8,128)S(1)}, f32[20,256]{1,0:T(8,128)}, u32[]{:S(2)}) copy-start(f32[20,256]{1,0:T(8,128)} %param.11) | copy-start | bytes 61444
  72.5 3.7 %copy-start.7 = (pred[256,256]{1,0:T(8,128)(4,1)S(1)}, pred[256,256]{1,0:T(8,128)(4,1)}, u32[]{:S(2)}) copy-start(pred[256,256]{1,0:T(8,128)(4,1)} %fusion.37) | copy-start | bytes 196612
  81.6 10.4 %copy-start.11 = (f32[20]{0:T(128)S(1)}, f32[20]{0:T(128)}, u32[]{:S(2)}) copy-start(f32[20]{0:T(128)} %copy-done.10) | copy-start | bytes 244
  81.6 10.4 %copy-start.12 = (f32[20]{0:T(128)S(1)}, f32[20]{0:T(128)}, u32[]{:S(2)}) copy-start(f32[20]{0:T(128)} %slice_reduce_fusion.1) | copy-start | bytes 244
  81.6 11.3 %copy-start.2 = (bf16[256,128]{1,0:T(8,128)(2,1)S(1)}, bf16[256,128]{1,0:T(8,128)(2,1)}, u32[]{:S(2)}) copy-start(bf16[256,128]{1,0:T(8,128)(2,1)} %param.13) | copy-start | bytes 196612
  88.2 6.8 %copy-start.14 = (f32[20]{0:T(128)S(1)}, f32[20]{0:T(128)}, u32[]{:S(2)}) copy-start(f32[20]{0:T(128)} %get-tuple-element.151) | copy-start | bytes 244
  88.2 6.8 %copy-start.15 = (f32[20]{0:T(128)S(1)}, f32[20]{0:T(128)}, u32[]{:S(2)}) copy-start(f32[20]{0:T(128)} %get-tuple-element.159) | copy-start | bytes 244
  88.2 27.8 %copy-start.4 = (bf16[256,128]{1,0:T(8,128)(2,1)S(1)}, bf16[256,128]{1,0:T(8,128)(2,1)}, u32[]{:S(2)}) copy-start(bf16[256,128]{1,0:T(8,128)(2,1)} %param.14) | copy-start | bytes 196612
  88.2 27.8 %copy-start.8 = (pred[256,256]{1,0:T(8,128)(4,1)S(1)}, pred[256,256]{1,0:T(8,128)(4,1)}, u32[]{:S(2)}) copy-start(pred[256,256]{1,0:T(8,128)(4,1)} %fusion.37) | copy-start | bytes 196612
